TPU v7x, 512 devices: a 8x2x16 block of a 8x8x16 slice. The times are simulated.
512 devices in a mesh: grp: 2 (over y), dp: 256 (over z, x, core).
Axes of the slice: x: 8, y: 2, z: 16, core: 2. Of those that a mesh axis runs over, the one named last changes fastest.
The devices are a block of a 8x8x16 slice.
Arguments:
- params: float32 [1900544], P(('grp', 'dp')), parts along dimension 0, may hold values from -0.3 to 0.3
- momentum: float32 [1900544], P(('grp', 'dp')), parts along dimension 0, may hold values from -6 to 6
- noise_draws: float32 [2, 950272], P('grp', 'dp'), parts along dimension 0, may hold values from -6 to 6
- images: float32 [262144, 448], P(('grp', 'dp')), parts along dimension 0, may hold values from -6 to 6
- labels: int32 [262144], P(('grp', 'dp')), parts along dimension 0, may hold values from 0 to 9
- indices: int32 [2, 65536], P('grp', 'dp'), parts along dimension 0, may hold values from 0 to 511
Outputs:
- params_out: float32 [1900544], P(('grp', 'dp')), parts along dimension 0
- momentum_out: float32 [1900544], P(('grp', 'dp')), parts along dimension 0
- losses: float32 [2], P('grp'), parts along dimension 0
There are 2 independent parts, one for each index of `grp`. A program takes and returns all parts, laid end to end along the dimension named above; each array names one. Nothing has to cross between parts.
All inputs are finite; a program needn't handle non-finite values.
Results may differ from a plain program's by a relative error of at most 0.0003.
Values sent between devices are 32-bit elements; how exact they have to be, the bound alone decides.
A program may use at most 64 MiB of HBM per device.

v0:
```python
import math

import jax
import jax.numpy as jnp
from jax import lax
from jax.sharding import Mesh
from jax.sharding import PartitionSpec as P

DIN = 448
H = 2048
OUT = 10
DP = ("dp_0", "dp_1", "dp_2")
GRP_DP = ("grp", "dp_0", "dp_1", "dp_2")


step_size = 0.02
friction = 15.0


def laid_out(parts, dim):
    dims = list(parts.shape[1:])
    dims[dim] *= parts.shape[0]
    return jnp.moveaxis(parts, 0, dim).reshape(dims)


def gather_in_order(value, axes, turns):
    parts = value[None]
    for k in turns:
        parts = lax.all_gather(parts, axes[k], axis=0, tiled=True)
    block = [lax.axis_size(axes[k]) for k in reversed(turns)]
    parts = parts.reshape(*block, *value.shape)
    turned = sorted(range(len(turns)), key=lambda place: turns[len(turns) - 1 - place])
    return parts.transpose(*turned, *range(len(turns), parts.ndim)).reshape(-1, *value.shape)


def gathered_by_axis(value, axes, turns, dim):
    return laid_out(gather_in_order(value, axes, turns), dim)


def one_axis_at_a_time(value, axes):
    for axis in axes:
        value = lax.psum(value, axis)
    return value


def own_block(parts, axes, turns):
    dims = [lax.axis_size(a) for a in axes]
    parts = parts.reshape(*dims, *parts.shape[1:])
    parts = parts.transpose(*turns, *range(len(axes), parts.ndim))
    parts = parts.reshape(-1, *parts.shape[len(axes) :])
    for k in turns:
        parts = lax.psum_scatter(parts, axes[k], scatter_dimension=0, tiled=True)
    return parts[0]


def cut_along(value, dim, size):
    before, after = (value.shape[:dim], value.shape[dim + 1 :])
    return jnp.moveaxis(value.reshape(*before, size, -1, *after), dim, 0)


def scatter_axes(value, axes, turns, dim):
    size = lax.axis_size(axes)
    return own_block(cut_along(value, dim, size), axes, turns)


def unpack(flat_vec):
    in_end = DIN * H
    w_in = flat_vec[:in_end].reshape(DIN, H)
    b_in = flat_vec[in_end : in_end + H]
    hid_end = in_end + H
    w_out = flat_vec[hid_end : hid_end + H * OUT].reshape(H, OUT)
    b_out = flat_vec[hid_end + H * OUT : hid_end + H * OUT + OUT]
    return (w_in, b_in, w_out, b_out)


def total_nll(flat_vec, chosen_rows, targets):
    w_in, b_in, w_out, b_out = unpack(flat_vec)
    hidden = jnp.tanh(
        jnp.dot(
            chosen_rows, w_in, precision=lax.Precision.HIGHEST, preferred_element_type=jnp.float32
        )
        + b_in
    )
    logits = (
        jnp.dot(hidden, w_out, precision=lax.Precision.HIGHEST, preferred_element_type=jnp.float32)
        + b_out
    )
    log_norm = jnp.log(jnp.sum(jnp.exp(logits), axis=1))
    classes = lax.broadcasted_iota(jnp.int32, logits.shape, 1)
    picked = jnp.sum(jnp.where(targets[:, None] == classes, logits, 0.0), axis=1)
    return jnp.sum(log_norm - picked)


def prior_precision(flat_index):
    in_end = DIN * H
    hid_end = in_end + H
    out_end = hid_end + H * OUT
    return jnp.where(
        flat_index < in_end,
        float(DIN),
        jnp.where(flat_index < hid_end, 1.0, jnp.where(flat_index < out_end, float(H), 1.0)),
    )


def body(params, momentum, noise_draws, images, labels, indices):
    shard_len = params.shape[0]
    shard_start = lax.axis_index(DP) * shard_len
    precision = prior_precision(shard_start + lax.iota(jnp.int32, shard_len))
    scale_data = images.shape[0] / indices.shape[1]
    row_count = lax.axis_size(DP) * indices.shape[1]
    gathered = gathered_by_axis(params, DP, (0, 1, 2), 0)
    picked_rows = indices[0]
    chosen_rows = jnp.take(images, picked_rows, axis=0)
    targets = jnp.take(labels, picked_rows, axis=0)
    nll_part, pullback = jax.vjp(
        lambda weights_flat: total_nll(weights_flat, chosen_rows, targets), gathered
    )
    (local_grad,) = pullback(jnp.ones_like(nll_part))
    losses = [one_axis_at_a_time(nll_part, DP) / row_count]
    own_grad = scatter_axes(local_grad, DP, (2, 0, 1), 0)
    total_force = scale_data * own_grad + precision * params
    momentum = (
        (1.0 - step_size * friction) * momentum
        - step_size * total_force
        + math.sqrt(2.0 * friction * step_size) * noise_draws[0]
    )
    params = params + step_size * momentum
    return (params, momentum, jnp.stack(losses))


def solution(mesh):
    torus = Mesh(mesh.devices.reshape(mesh.shape["grp"], 16, 8, 2), ("grp", "dp_0", "dp_1", "dp_2"))
    placed = (P(GRP_DP), P(GRP_DP), P("grp", DP), P(GRP_DP, None), P(GRP_DP), P("grp", DP))
    return jax.shard_map(
        body,
        mesh=torus,
        in_specs=placed,
        out_specs=(P(GRP_DP), P(GRP_DP), P("grp")),
        check_vma=False,
    )
```

profile of v0, /device:TPU:65, one launch (start us, length us, event | category | flops | bytes accessed | tf_op | source)
XLA Modules:
  0.0 465.7 jit_solution(17000663822888148046)
XLA Ops:
  7.2 0.0 copy-start
  7.2 0.1 all-gather.5.cloned.1.call-start
  7.3 0.8 reshape.105
  8.1 63.2 %all-gather.1 = f32[16,1,3712]{2,1,0:T(1,128)S(1)} all-gather(f32[1,1,3712]{2,1,0:T(1,128)S(1)} %reshape.105), channel_id=2, replica_groups=mesh['grp'=2,'dp_0'=16,'dp_1'=8,'dp_2'=2] {'dp_0'}, dimensions={0}, use_global_device_ids=true | all-gather | bytes 252416 | tf_op jit(solution)/shard_map/all_gather | solution.py:29
  71.2 0.7 copy.26
  71.9 0.1 all-gather.5.cloned.1.call-update
  72.0 0.1 all-gather.7.cloned.1.call-start
  72.1 43.2 %all-gather.5.cloned.1.call-done = f32[128,3712]{1,0:T(8,128)} async-done(((f32[16,3712]{1,0:T(8,128)}), f32[128,3712]{1,0:T(8,128)}) %all-gather.5.cloned.1.call-update) | async-done | bytes 1900560 | tf_op jit(solution)/shard_map/all_gather | solution.py:29
  115.2 0.1 all-gather.7.cloned.1.call-update
  115.3 0.1 reduce-scatter.2.cloned.1.call-start
  115.4 0.3 copy.17
  115.7 1.0 gather_fusion.1
  116.7 1.9 gather_fusion
  118.7 29.5 %all-gather.7.cloned.1.call-done = f32[256,3712]{1,0:T(8,128)} async-done(((f32[128,3712]{1,0:T(8,128)}), f32[256,3712]{1,0:T(8,128)}) %all-gather.7.cloned.1.call-update) | async-done | bytes 3801104 | tf_op jit(solution)/shard_map/all_gather | solution.py:29
  148.2 6.8 %copy.18 = f32[16,8,2,3712]{3,2,1,0:T(2,128)} copy(f32[16,8,2,3712]{3,0,1,2:T(8,128)} %bitcast.26) | data formatting | bytes 7602176 | tf_op jit(solution)/shard_map/transpose | solution.py:33
  155.0 5.8 %slice.15 = f32[464,2048]{1,0:T(8,128)} reshape(f32[16,8,2,3712]{3,2,1,0:T(2,128)} %copy.18) | data formatting | bytes 7602176 | tf_op jit(solution)/shard_map/jvp()/slice | solution.py:68
  160.8 5.9 %reshape_reshape.6 = f32[950272]{0:T(1024)} reshape(f32[16,8,2,3712]{3,2,1,0:T(2,128)} %copy.18) | data formatting | bytes 7602176 | tf_op jit(solution)/shard_map/reshape;reshape | solution.py:23
  166.8 0.7 slice.25
  167.5 0.9 slice.26
  168.3 1.1 reshape.84
  169.4 5.7 %fusion.5 = f32[256,2048]{1,0:T(8,128)S(1)} fusion(f32[464,2048]{1,0:T(8,128)} %slice.15, f32[2048]{0:T(1024)S(1)} %slice.25, f32[256,448]{1,0:T(8,128)S(1)} %gather_fusion.1, pred[256]{0:T(512)(128)(4,1)S(1)} %get-tuple-element.8), kind=kOutput, calls=%fused_computation.6 | convolution fusion | flops 2819211264 | bytes 6234368 | tf_op jit(solution)/shard_map/jvp()/dot_general | solution.py:79
  175.1 1.9 exponential_reduce_fusion
  177.0 2.1 fusion.26
  179.1 3.6 fusion.18
  182.7 0.1 select_reduce_fusion
  182.9 3.6 convolution_bitcast_fusion
  186.5 2.6 copy.24
  189.1 0.8 reshape.85
  189.9 4.1 pad_add_fusion
  194.0 5.5 %reshape_reshape.7 = f32[16,8,2,3712]{3,2,1,0:T(2,128)} reshape(f32[950272]{0:T(1024)} %pad_add_fusion) | data formatting | bytes 7602176 | tf_op jit(solution)/shard_map/reshape;reshape | solution.py:48
  199.5 4.1 copy.21
  203.6 0.1 reduce-scatter.2.cloned.1.call-update
  203.7 0.1 all-reduce.9.cloned.1.call-start
  203.8 24.2 %reduce-scatter.2.cloned.1.call-done = f32[128,3712]{1,0:T(8,128)} async-done(((f32[256,3712]{1,0:T(8,128)}), f32[128,3712]{1,0:T(8,128)}) %reduce-scatter.2.cloned.1.call-update) | async-done | bytes 1900560 | tf_op jit(solution)/shard_map/reduce_scatter | solution.py:52
  228.0 0.1 all-reduce.9.cloned.1.call-update
  228.1 0.1 all-reduce.11.cloned.1.call-start
  228.1 1.3 dynamic-slice
  230.1 138.7 %all-reduce.9.cloned.1.call-done = f32[128,3712]{1,0:T(8,128)} async-done(((f32[128,3712]{1,0:T(8,128)}), f32[128,3712]{1,0:T(8,128)}) %all-reduce.9.cloned.1.call-update) | async-done | bytes 1900560
  368.8 1.6 constant_dynamic-slice_fusion
  370.3 0.1 all-reduce.11.cloned.1.call-update
  370.5 1.3 dynamic-slice.2
  371.7 0.6 subtract_reduce_fusion
  372.3 21.5 %psum.21 = f32[]{:T(128)} all-reduce(f32[]{:T(128)} %subtract_reduce_fusion), channel_id=1, replica_groups=mesh['grp'=2,'dp_0'=16,'dp_1'=8,'dp_2'=2] {'dp_0'}, use_global_device_ids=true, to_apply=%region_8.9 | all-reduce | flops 1 | bytes 8 | tf_op jit(solution)/shard_map/psum | solution.py:42
  393.8 14.4 %psum.22 = f32[]{:T(128)} all-reduce(f32[]{:T(128)} %psum.21), channel_id=1, replica_groups=mesh['grp'=2,'dp_0'=16,'dp_1'=8,'dp_2'=2] {'dp_1'}, use_global_device_ids=true, to_apply=%region_9.10 | all-reduce | flops 1 | bytes 8 | tf_op jit(solution)/shard_map/psum | solution.py:42
  408.2 23.8 %psum.23 = f32[]{:T(128)} all-reduce(f32[]{:T(128)} %psum.22), channel_id=1, replica_groups=mesh['grp'=2,'dp_0'=16,'dp_1'=8,'dp_2'=2] {'dp_2'}, use_global_device_ids=true, to_apply=%region_10.11 | all-reduce | flops 1 | bytes 8 | tf_op jit(solution)/shard_map/psum | solution.py:42
  432.7 23.1 %all-reduce.11.cloned.1.call-done = f32[8,3712]{1,0:T(8,128)} async-done(((f32[8,3712]{1,0:T(8,128)}), f32[8,3712]{1,0:T(8,128)}) %all-reduce.11.cloned.1.call-update) | async-done | bytes 118800
  455.8 1.6 fusion.17
  457.4 0.6 multiply_add_fusion
  (18 shorter events, 0.1 us)
Async XLA Ops:
  7.2 109.5 %copy-start = (s32[512]{0:T(512)S(1)}, s32[512]{0:T(512)}, u32[]{:S(2)}) copy-start(s32[512]{0:T(512)} %param.10) | copy-start | bytes 6148
  7.2 108.2 %copy-start.1 = (f32[512,448]{0,1:T(8,128)S(1)}, f32[512,448]{0,1:T(8,128)}, u32[]{:S(2)}) copy-start(f32[512,448]{0,1:T(8,128)} %param.9) | copy-start | bytes 2752516
  7.2 108.0 %all-gather.5.cloned.1.call-start = ((), (), s32[]{:S(2)}) async-start(), calls=%async_computation.1 | async-start | bytes 2138112 | tf_op jit(solution)/shard_map/all_gather | solution.py:29
  71.9 43.8 %copy-start.5 = (s32[1,256]{1,0:T(1,128)S(1)}, s32[1,256]{1,0:T(1,128)}, u32[]{:S(2)}) copy-start(s32[1,256]{1,0:T(1,128)} %param.11) | copy-start | bytes 3076
  72.0 76.2 %all-gather.7.cloned.1.call-start = ((), (), s32[]{:S(2)}) async-start(), calls=%async_computation.2 | async-start | bytes 5701632 | tf_op jit(solution)/shard_map/all_gather | solution.py:29
  115.3 112.7 %reduce-scatter.2.cloned.1.call-start = ((), (), s32[]{:S(2)}) async-start(), calls=%async_computation.3 | async-start | bytes 5701632 | tf_op jit(solution)/shard_map/reduce_scatter | solution.py:52
  169.4 5.7 %slice-start = ((f32[950272]{0:T(1024)}), f32[10]{0:T(128)S(1)}, s32[]{:S(2)}) async-start(f32[950272]{0:T(1024)} %reshape_reshape.6), calls=%async_computation.6 | async-start | bytes 1024 | tf_op jit(solution)/shard_map/jvp()/slice | solution.py:72
  203.7 166.7 %copy-start.4 = (f32[1,3712]{1,0:T(1,128)S(1)}, f32[1,3712]{1,0:T(1,128)}, u32[]{:S(2)}) copy-start(f32[1,3712]{1,0:T(1,128)} %param.8) | copy-start | bytes 44548
  203.7 253.7 %copy-start.2 = (f32[3712]{0:T(1024)S(1)}, f32[3712]{0:T(1024)}, u32[]{:S(2)}) copy-start(f32[3712]{0:T(1024)} %param.6) | copy-start | bytes 44548
  203.7 253.7 %copy-start.3 = (f32[3712]{0:T(1024)S(1)}, f32[3712]{0:T(1024)}, u32[]{:S(2)}) copy-start(f32[3712]{0:T(1024)} %param.7) | copy-start | bytes 44548
  203.7 165.0 %all-reduce.9.cloned.1.call-start = ((), (), s32[]{:S(2)}) async-start(), calls=%async_computation.4 | async-start | bytes 3801088
  228.1 227.7 %all-reduce.11.cloned.1.call-start = ((), (), s32[]{:S(2)}) async-start(), calls=%async_computation.5 | async-start | bytes 237568
Sparse Core Ops, SparseCore 0:
  72.1 43.0 all-gather.4
  117.3 30.7 all-gather.6
  203.8 24.1 reduce-scatter.1
  230.3 138.4 all-reduce.8
  371.0 84.7 all-reduce.10
where the time goes:
time: 470 us; the launch traced here: 466 us
  waiting for transfers between devices  259 us (55%)
  blocking collectives  123 us (26%)
  local copies, waits for them, and re-layouts  43.1 us (9%)
  matrix products  16.9 us (4%)
  between operations  16.5 us (4%)
  other arithmetic  7.13 us (2%)
    unnamed x7, waiting for transfers between devices  162 us
    all_gather x2, waiting for transfers between devices, gather_in_order(): parts = lax.all_gather(parts, axes[k], axis=0, tiled=True)  72.6 us
    all_gather x1, blocking collectives, gather_in_order(): parts = lax.all_gather(parts, axes[k], axis=0, tiled=True)  63.2 us
    psum x3, blocking collectives, one_axis_at_a_time(): value = lax.psum(value, axis)  59.7 us
    reduce_scatter x1, waiting for transfers between devices, own_block(): parts = lax.psum_scatter(parts, axes[k], scatter_dimension=0, tiled=True)  24.2 us
  transfers between devices with their start and end apart: 5, of which 5 were waited for; matrix products, arithmetic and copies ran while one was open for 1% of the time, Pallas kernels for 0%

commit v1 on v0

v1 whole, which is shorter than its diff:
```python
import functools
import math

import jax
import jax.numpy as jnp
from jax import lax
from jax.experimental import pallas as pl
from jax.experimental.pallas import tpu as pltpu
from jax.sharding import Mesh
from jax.sharding import PartitionSpec as P

DIN = 448
H = 2048
OUT = 10
NZ, NX, NC = 16, 8, 2
LANES = 128
ROW = H // LANES
HALF = ROW // 2
HID = H // 2
ZROWS = 29
ZPAD = 32
BLK = ZPAD * HALF
SUB0 = 15 * HALF
KPAD = 16
W2L = HID * OUT // LANES
DP = ("dp_0", "dp_1", "dp_2")
GRP_DP = ("grp", "dp_0", "dp_1", "dp_2")
MESH = pl.DeviceIdType.MESH
F32 = jnp.float32
BF16 = jnp.bfloat16

step_size = 0.02
friction = 15.0


def split(value):
    high = value.astype(BF16)
    return high, (value - high.astype(F32)).astype(BF16)


def dot(a, b):
    return jnp.dot(a, b, preferred_element_type=F32)


def dot_nt(a, b):
    return lax.dot_general(a, b, (((1,), (1,)), ((), ())), preferred_element_type=F32)


def iota(shape, dim):
    return lax.broadcasted_iota(jnp.int32, shape, dim)


def tenth(e):
    return (e * 6554) >> 16


def kernel(
    nz, nx, slot, lines, tail_z, tail_r,
    par, idx, lab, img_any, out,
    img, xs, ys, xh, xl, xth, xtl, slots, zrow, gh, tp, tt, hidf, hidh, hidl, lg, w48, dl48, dwl, ep, ee,
    d2, rb, pk, sx, rx,
    img_sem, dd_send, dd_recv, xs_send, xf_send, xs_recv, zs_send, zs_recv, rs_send, rs_recv, rx_send, rx_recv,
):
    batch = idx.shape[1]
    pool = lab.shape[1]
    din = img.shape[1]
    kdim = nz * ZPAD
    g, z, x, c = (lax.axis_index(a) for a in GRP_DP)
    oc = 1 - c
    partner = (g, z, x, oc)
    zside = ((g, lax.rem(z + 1, nz), x, c), (g, lax.rem(z + nz - 1, nz), x, c))
    half_nz = nz // 2

    def zmod(v):
        return lax.rem(v + 2 * nz, nz)

    def xpos(dx):
        return lax.rem(x + dx, nx)

    deltas = []
    for d in range(1, nx // 2 + 1):
        for v in (d, nx - d):
            if v not in deltas:
                deltas.append(v)

    image_copy = pltpu.make_async_copy(img_any, img, img_sem)
    image_copy.start()

    barrier = pltpu.get_barrier_semaphore()
    peers = [partner, zside[0], zside[1]] + [(g, z, xpos(d), c) for d in deltas]
    for peer in peers:
        pl.semaphore_signal(barrier, inc=1, device_id=peer, device_id_type=MESH)

    zeros_pad = jnp.zeros((BLK - ZROWS * HALF, LANES), F32)
    for zz in range(nz):
        gh[zz * BLK + ZROWS * HALF : (zz + 1) * BLK, :] = zeros_pad

    def remote(src, dst, send, recv, to):
        return pltpu.make_async_remote_copy(
            src_ref=src, dst_ref=dst, send_sem=send, recv_sem=recv, device_id=to, device_id_type=MESH
        )

    def at(ref, start, size, step=8):
        return ref.at[pl.ds(pl.multiple_of(start, step), size)]

    pl.semaphore_wait(barrier, len(peers))

    mine = 2 * x + c

    def place(k):
        return at(slots, k * slot, slot)

    x_sends = []
    for i, d in enumerate(deltas):
        x_sends.append(remote(par, place(mine), xs_send.at[i], xs_recv.at[mine], (g, z, xpos(d), c)))
    x_sends.append(remote(par, place(mine), xs_send.at[nx - 1], xs_recv.at[mine], partner))
    for copy in x_sends:
        copy.start()
    slots[pl.ds(pl.multiple_of(mine * slot, 8), slot), :] = par[...]

    image_copy.wait()
    hot_t = (iota((pool, batch), 0) == idx[...]).astype(F32)
    hot = hot_t.T.astype(BF16)
    q = iota((din, kdim), 1)
    spread = ((q & (ZPAD - 1)) < ZROWS) & (iota((din, kdim), 0) == (q >> 5) * ZROWS + (q & (ZPAD - 1)))
    spread = spread.astype(F32).astype(BF16)
    img_h, img_l = split(img[...])
    rows = dot(dot(hot, img_h).astype(BF16), spread) + dot(dot(hot, img_l).astype(BF16), spread)
    rows = rows + (iota((batch, kdim), 1) == tail_z * ZPAD + tail_r).astype(F32)
    xs[pl.ds(pl.multiple_of(c * batch, 8), batch), :] = rows
    lab_hot = (iota((KPAD, pool), 0) == lab[...]).astype(F32).astype(BF16)
    ys[pl.ds(pl.multiple_of(c * KPAD, 8), KPAD), :] = dot(lab_hot, hot_t.astype(BF16))
    row_copy = remote(at(xs, c * batch, batch), at(xs, c * batch, batch), dd_send.at[0], dd_recv.at[0], partner)
    hot_copy = remote(at(ys, c * KPAD, KPAD), at(ys, c * KPAD, KPAD), dd_send.at[1], dd_recv.at[1], partner)

    def arrived(k, i, to):
        return remote(place(k), place(k), xf_send.at[i], xs_recv.at[k], to)

    forwards = []
    for i, d in enumerate(deltas):
        k = 2 * xpos(d) + c
        copy = arrived(k, i, partner)
        copy.wait_recv()
        copy.start()
        forwards.append(copy)
    row_copy.start()
    hot_copy.start()
    for i, d in enumerate([0] + deltas):
        k = 2 * xpos(d) + oc
        arrived(k, 0, partner).wait_recv()
    for k in range(2 * nx):
        zrow[lines * k : lines * (k + 1), :] = slots[slot * k : slot * k + lines, :]
    for r in range(ZROWS):
        gh[pl.ds(pl.multiple_of(z * BLK + HALF * r, 8), HALF), :] = zrow[
            pl.ds(pl.multiple_of(ROW * r + HALF * c, 8), HALF), :
        ]

    sub_size = (SUB0, ZROWS * HALF - SUB0)

    def ag(way, hop, sub, back):
        sign = 1 if way == 0 else -1
        block = zmod(z - sign * (hop - 1 + back))
        ref = at(gh, block * BLK + sub * SUB0, sub_size[sub])
        return remote(ref, ref, zs_send.at[way, hop - 1, sub], zs_recv.at[way, hop - 1, sub], zside[way])

    def each(fn):
        for sub in range(2):
            for way in range(2):
                fn(way, sub)

    each(lambda way, sub: ag(way, 1, sub, 0).start())

    row_copy.wait_recv()
    hot_copy.wait_recv()
    for part in range(2 * batch // 128):
        span = slice(128 * part, 128 * (part + 1))
        value = xs[span, :]
        xh[span, :], xl[span, :] = split(value)
        xth[:, span], xtl[:, span] = split(value.T)

    def ag_hop(hop, _):
        def one(way, sub):
            ag(way, hop - 1, sub, 1).wait_recv()
            ag(way, hop, sub, 0).start()

        each(one)
        return 0

    lax.fori_loop(2, half_nz, ag_hop, 0)
    each(lambda way, sub: ag(way, half_nz - 1, sub, 1).wait_recv())
    for way in range(2):
        ag(way, half_nz, way, 0).start()
    for way in range(2):
        ag(way, half_nz, way, 1).wait_recv()

    tail = tail_z * BLK + tail_r * HALF
    tail_copy = remote(gh.at[tail : tail + 12 * HALF], tp, dd_send.at[2], dd_recv.at[2], partner)
    tail_copy.start()

    def forward(n, _):
        w = jnp.concatenate(
            [gh[pl.ds(2 * n, kdim, stride=HALF), :], gh[pl.ds(2 * n + 1, kdim, stride=HALF), :]], axis=1
        )
        wh, wl = split(w)
        pre = dot(xh[...], wh) + dot(xh[...], wl) + dot(xl[...], wh)
        hid = jnp.tanh(pre)
        span = pl.ds(pl.multiple_of(256 * n, 256), 256)
        hidf[:, span] = hid
        hidh[:, span], hidl[:, span] = split(hid)
        return 0

    lax.fori_loop(0, HID // 256, forward, 0)

    tail_copy.wait_recv()
    for r in range(12):
        tt[pl.ds(pl.multiple_of(ROW * r + HALF * c, 8), HALF), :] = gh[tail + HALF * r : tail + HALF * (r + 1), :]
        tt[pl.ds(pl.multiple_of(ROW * r + HALF * oc, 8), HALF), :] = tp[HALF * r : HALF * (r + 1), :]
    dwl[...] = tt[pl.ds(pl.multiple_of(ROW + W2L * c, 8), W2L), :]
    groups = HID // LANES
    pieces = []
    for i in range(OUT):
        e = iota((KPAD, LANES), 1) + LANES * i
        keep = (e - OUT * tenth(e)) == iota((KPAD, LANES), 0)
        line = dwl[pl.ds(i, groups, stride=OUT), :]
        spread_line = jnp.where(keep[None], line[:, None, :], 0.0)
        pieces.append(spread_line.reshape(groups * KPAD, LANES))
    wide_h, wide_l = split(jnp.concatenate(pieces, axis=1))
    pick = (tenth(iota((OUT * LANES, LANES), 0)) == iota((OUT * LANES, LANES), 1)).astype(F32).astype(BF16)
    w2b = dot(wide_h, pick) + dot(wide_l, pick)
    w2t = jnp.concatenate([w2b[KPAD * m : KPAD * (m + 1), :] for m in range(groups)], axis=1)
    w2h, w2l = split(w2t)
    w48[...] = jnp.concatenate([w2h, w2l, w2h], axis=0)
    both = dot_nt(w48[0 : 2 * KPAD, :], hidh[...])
    part_logits = both[:KPAD] + both[KPAD:] + dot_nt(w48[0:KPAD, :], hidl[...])
    lg[pl.ds(pl.multiple_of(c * KPAD, 8), KPAD), :] = part_logits
    logit_copy = remote(at(lg, c * KPAD, KPAD), at(lg, c * KPAD, KPAD), dd_send.at[3], dd_recv.at[3], partner)
    logit_copy.start()
    b2_line = tt[ROW + 2 * W2L : ROW + 2 * W2L + 1, :]
    b2 = jnp.sum(jnp.where(iota((KPAD, LANES), 0) == iota((KPAD, LANES), 1), b2_line, 0.0), axis=1, keepdims=True)
    real = iota((KPAD, 2 * batch), 0) < OUT
    b2 = jnp.where(iota((KPAD, 1), 0) < OUT, b2, 0.0)
    targets = jnp.concatenate([ys[0:KPAD, :], ys[KPAD : 2 * KPAD, :]], axis=1)
    logit_copy.wait_recv()
    logits = lg[0:KPAD, :] + lg[KPAD : 2 * KPAD, :] + b2
    expo = jnp.where(real, jnp.exp(logits), 0.0)
    norm = jnp.sum(expo, axis=0, keepdims=True)
    picked = jnp.sum(targets * logits, axis=0, keepdims=True)
    nll = jnp.sum(jnp.log(norm) - picked, axis=1, keepdims=True)
    dlog = expo / norm - targets
    dlh, dll = split(dlog)
    dl3 = jnp.concatenate([dlh.astype(F32), dlh.astype(F32), dll.astype(F32)], axis=0)
    dl48[...] = dl3.T.astype(BF16)

    dlhl = jnp.concatenate([dlh, dll], axis=0)
    both = dot(dlhl, hidh[...])
    dw2t = both[:KPAD] + both[KPAD:] + dot(dlh, hidl[...])
    dw2b = jnp.concatenate([dw2t[:, LANES * m : LANES * (m + 1)] for m in range(groups)], axis=0)
    dwh, dwlo = split(dw2b)
    e = iota((LANES, OUT * LANES), 1)
    place_back = (tenth(e) == iota((LANES, OUT * LANES), 0)).astype(F32).astype(BF16)
    flat = dot(dwh, place_back) + dot(dwlo, place_back)
    e = iota((groups * KPAD, OUT * LANES), 1)
    flat = jnp.where((e - OUT * tenth(e)) == (iota((groups * KPAD, OUT * LANES), 0) & (KPAD - 1)), flat, 0.0)
    flat = jnp.sum(flat.reshape(groups, KPAD, OUT * LANES), axis=1)
    for i in range(OUT):
        dwl[pl.ds(i, groups, stride=OUT), :] = flat[:, LANES * i : LANES * (i + 1)]
    grad_copy = remote(dwl, ep, dd_send.at[4], dd_recv.at[4], partner)
    grad_copy.start()
    ee[2 * W2L : 2 * W2L + ROW, :] = jnp.zeros((ROW, LANES), F32)
    db2 = jnp.sum(dlog, axis=1, keepdims=True)
    ee[2 * W2L : 2 * W2L + 1, :] = jnp.sum(
        jnp.where(iota((KPAD, LANES), 0) == iota((KPAD, LANES), 1), db2, 0.0), axis=0, keepdims=True
    )
    ee[pl.ds(pl.multiple_of(W2L * c, 8), W2L), :] = dwl[...]

    def backward(n, _):
        span = pl.ds(pl.multiple_of(256 * n, 256), 256)
        h = hidf[:, span]
        dh, dl = split(dot(dl48[...], w48[:, span]) * (1.0 - h * h))
        grad = dot(xth[...], dh) + dot(xth[...], dl) + dot(xtl[...], dh)
        d2[pl.ds(2 * n, kdim, stride=HALF), :] = grad[:, :LANES]
        d2[pl.ds(2 * n + 1, kdim, stride=HALF), :] = grad[:, LANES:]
        return 0

    lax.fori_loop(0, HID // 256, backward, 0)
    nll_lines = jnp.broadcast_to(nll, (HALF, LANES))
    for zz in range(nz):
        d2[zz * BLK + ZROWS * HALF : zz * BLK + (ZROWS + 1) * HALF, :] = nll_lines
    grad_copy.wait_recv()
    ee[pl.ds(pl.multiple_of(W2L * oc, 8), W2L), :] = ep[...]
    for r in range(11):
        d2[tail + HALF * (r + 1) : tail + HALF * (r + 2), :] = ee[pl.ds(pl.multiple_of(ROW * r + HALF * c, 8), HALF), :]

    def rs(way, hop, sub, back):
        sign = 1 if way == 0 else -1
        block = zmod(z + sign * (half_nz + 1 - hop - back))
        src = at(d2, block * BLK + sub * SUB0, SUB0)
        dst = at(rb, ((way * half_nz + hop - 1) * 2 + sub) * SUB0, SUB0)
        return remote(src, dst, rs_send.at[way, hop - 1, sub], rs_recv.at[way, hop - 1, sub], zside[way])

    def add_arrived(way, hop, sub):
        sign = 1 if way == 0 else -1
        rs(way, hop, sub, 0).wait_recv()
        block = zmod(z + sign * (half_nz - hop))
        span = pl.ds(pl.multiple_of(block * BLK + sub * SUB0, 8), SUB0)
        got = pl.ds(pl.multiple_of(((way * half_nz + hop - 1) * 2 + sub) * SUB0, 8), SUB0)
        d2[span, :] = d2[span, :] + rb[got, :]

    for way in range(2):
        rs(way, 1, way, 0).start()
    for way in range(2):
        rs(way, 2, 1 - way, 0).start()
    for way in range(2):
        add_arrived(way, 1, way)
        rs(way, 2, way, 0).start()

    def rs_hop(hop, _):
        def one(way, sub):
            add_arrived(way, hop - 1, sub)
            rs(way, hop, sub, 0).start()

        each(one)
        return 0

    lax.fori_loop(3, half_nz + 1, rs_hop, 0)
    each(lambda way, sub: add_arrived(way, half_nz, sub))

    own = at(d2, z * BLK, 2 * SUB0)
    swap = remote(own, pk, dd_send.at[5], dd_recv.at[5], partner)
    swap.start()
    for r in range(ZROWS):
        zrow[pl.ds(pl.multiple_of(ROW * r + HALF * c, 8), HALF), :] = d2[
            pl.ds(pl.multiple_of(z * BLK + HALF * r, 8), HALF), :
        ]
    loss_line = d2[pl.ds(pl.multiple_of(z * BLK + HALF * ZROWS, 8), 8), :]
    swap.wait_recv()
    for r in range(ZROWS):
        zrow[pl.ds(pl.multiple_of(ROW * r + HALF * oc, 8), HALF), :] = pk[HALF * r : HALF * (r + 1), :]
    for core in range(2):

        @pl.when(c == core)
        def _():
            for k in range(nx):
                first = lines * (2 * k + core)
                sx[slot * k : slot * k + lines, :] = zrow[first : first + lines, :]
                sx[slot * k + lines : slot * k + lines + 1, :] = loss_line[0:1, :]

    finals = []
    for i, d in enumerate(deltas):
        to = xpos(d)
        finals.append(
            remote(at(sx, to * slot, slot), at(rx, x * slot, slot), rx_send.at[i], rx_recv.at[x], (g, z, to, c))
        )
    for copy in finals:
        copy.start()
    total = sx[pl.ds(pl.multiple_of(x * slot, 8), slot), :]
    for i, d in enumerate(deltas):
        source = xpos(d)
        remote(at(sx, source * slot, slot), at(rx, source * slot, slot), rx_send.at[i], rx_recv.at[source], partner).wait_recv()
        total = total + rx[pl.ds(pl.multiple_of(source * slot, 8), slot), :]
    out[...] = total

    for copy in x_sends + forwards + [row_copy, hot_copy, tail_copy, logit_copy, grad_copy, swap] + finals:
        copy.wait_send()

    def drain(hop, _):
        each(lambda way, sub: ag(way, hop, sub, 0).wait_send())
        each(lambda way, sub: rs(way, hop + 1, sub, 0).wait_send())
        return 0

    lax.fori_loop(1, half_nz, drain, 0)
    for way in range(2):
        ag(way, half_nz, way, 0).wait_send()
        rs(way, 1, way, 0).wait_send()


def summed_gradient(shard, picked, labels, images, nz, nx):
    lines = shard.shape[0] // LANES
    slot = -(-(lines + 1) // 8) * 8
    batch, pool, din = picked.shape[1], images.shape[0], images.shape[1]
    kdim = nz * ZPAD
    half_nz = nz // 2
    padded = jnp.pad(shard, (0, slot * LANES - shard.shape[0])).reshape(slot, LANES)
    vmem = pl.BlockSpec(memory_space=pltpu.VMEM)
    dma = pltpu.SemaphoreType.DMA
    tail_z, tail_r = divmod(din, ZROWS)
    return pl.pallas_call(
        functools.partial(kernel, nz, nx, slot, lines, tail_z, tail_r),
        out_shape=jax.ShapeDtypeStruct((slot, LANES), F32),
        in_specs=[vmem, vmem, vmem, pl.BlockSpec(memory_space=pl.ANY)],
        out_specs=vmem,
        scratch_shapes=[
            pltpu.VMEM((pool, din), F32),
            pltpu.VMEM((2 * batch, kdim), F32),
            pltpu.VMEM((2 * KPAD, batch), F32),
            pltpu.VMEM((2 * batch, kdim), BF16),
            pltpu.VMEM((2 * batch, kdim), BF16),
            pltpu.VMEM((kdim, 2 * batch), BF16),
            pltpu.VMEM((kdim, 2 * batch), BF16),
            pltpu.VMEM((2 * nx * slot, LANES), F32),
            pltpu.VMEM((ZROWS * ROW, LANES), F32),
            pltpu.VMEM((nz * BLK, LANES), F32),
            pltpu.VMEM((12 * HALF, LANES), F32),
            pltpu.VMEM((12 * ROW, LANES), F32),
            pltpu.VMEM((2 * batch, HID), F32),
            pltpu.VMEM((2 * batch, HID), BF16),
            pltpu.VMEM((2 * batch, HID), BF16),
            pltpu.VMEM((2 * KPAD, 2 * batch), F32),
            pltpu.VMEM((3 * KPAD, HID), BF16),
            pltpu.VMEM((2 * batch, 3 * KPAD), BF16),
            pltpu.VMEM((W2L, LANES), F32),
            pltpu.VMEM((W2L, LANES), F32),
            pltpu.VMEM((2 * W2L + ROW, LANES), F32),
            pltpu.VMEM((nz * BLK, LANES), F32),
            pltpu.VMEM((2 * half_nz * 2 * SUB0, LANES), F32),
            pltpu.VMEM((2 * SUB0, LANES), F32),
            pltpu.VMEM((nx * slot, LANES), F32),
            pltpu.VMEM((nx * slot, LANES), F32),
            dma,
            dma((6,)),
            dma((6,)),
            dma((nx,)),
            dma((nx,)),
            dma((2 * nx,)),
            dma((2, half_nz, 2)),
            dma((2, half_nz, 2)),
            dma((2, half_nz, 2)),
            dma((2, half_nz, 2)),
            dma((nx,)),
            dma((nx,)),
        ],
        compiler_params=pltpu.CompilerParams(
            collective_id=0, has_side_effects=True, vmem_limit_bytes=56 * 1024 * 1024
        ),
    )(padded, picked, labels.reshape(1, -1), images)


def prior_precision(flat_index):
    in_end = DIN * H
    hid_end = in_end + H
    out_end = hid_end + H * OUT
    return jnp.where(
        flat_index < in_end,
        float(DIN),
        jnp.where(flat_index < hid_end, 1.0, jnp.where(flat_index < out_end, float(H), 1.0)),
    )


def body(params, momentum, noise_draws, images, labels, indices):
    shard_len = params.shape[0]
    shard_start = lax.axis_index(DP) * shard_len
    precision = prior_precision(shard_start + lax.iota(jnp.int32, shard_len))
    scale_data = images.shape[0] / indices.shape[1]
    row_count = lax.axis_size(DP) * indices.shape[1]
    summed = summed_gradient(params, indices, labels, images, lax.axis_size("dp_0"), lax.axis_size("dp_1"))
    lines = shard_len // LANES
    own_grad = summed[:lines].reshape(shard_len)
    losses = summed[lines, 0:1] / row_count
    total_force = scale_data * own_grad + precision * params
    momentum = (
        (1.0 - step_size * friction) * momentum
        - step_size * total_force
        + math.sqrt(2.0 * friction * step_size) * noise_draws[0]
    )
    params = params + step_size * momentum
    return (params, momentum, losses)


def solution(mesh):
    torus = Mesh(mesh.devices.reshape(mesh.shape["grp"], NZ, NX, NC), GRP_DP)
    placed = (P(GRP_DP), P(GRP_DP), P("grp", DP), P(GRP_DP, None), P(GRP_DP), P("grp", DP))
    return jax.shard_map(
        body,
        mesh=torus,
        in_specs=placed,
        out_specs=(P(GRP_DP), P(GRP_DP), P("grp")),
        check_vma=False,
    )
```

time: 470 us -> 142 us (0.30)
  waiting for transfers between devices: 259 us -> 0 us
  Pallas kernels: 0 us -> 134 us
  blocking collectives: 123 us -> 0 us
  local copies, waits for them, and re-layouts: 43.1 us -> 4.27 us
  matrix products: 16.9 us -> 0 us
  between operations: 16.5 us -> 2.47 us
  other arithmetic: 7.13 us -> 0.67 us
    unnamed x7 -> x0, waiting for transfers between devices: 162 us -> none
    pallas_call x0 -> x1, Pallas kernels: none -> 134 us  [summed_gradient(): pl.pallas_call(functools.partial(kernel, nz, nx, slot, lines, tail_z, tai...]
    all_gather x2 -> x0, waiting for transfers between devices: 72.6 us -> none  [gather_in_order(): parts = lax.all_gather(parts, axes[k], axis=0, tiled=True)]
    all_gather x1 -> x0, blocking collectives: 63.2 us -> none  [gather_in_order(): parts = lax.all_gather(parts, axes[k], axis=0, tiled=True)]
    psum x3 -> x0, blocking collectives: 59.7 us -> none  [one_axis_at_a_time(): value = lax.psum(value, axis)]
    reduce_scatter x1 -> x0, waiting for transfers between devices: 24.2 us -> none  [own_block(): parts = lax.psum_scatter(parts, axes[k], scatter_dimension=0, tiled=True)]
    dot_general x5 -> x0, matrix products: 16.9 us -> none  [the longest x2 9.32 us: total_nll(): jnp.dot(chosen_rows, w_in, precision=lax.Precision.HIGHEST, preferred_ele...]
    another operation x2 -> x0, local copies, waits for them, and re-layouts: 11.4 us -> none  [the longest x1 5.93 us: laid_out(): return jnp.moveaxis(parts, 0, dim).reshape(dims)]
  transfers between devices with their start and end apart: 5 -> 0, of which waited for: 5 -> 0; matrix products, arithmetic and copies ran while one was open for 1% -> 0% of each run, Pallas kernels for 0% -> 0%
where the time goes in v1:
time: 142 us; the launch traced here: 141 us
  Pallas kernels  134 us (94%)
  local copies, waits for them, and re-layouts  4.27 us (3%)
  between operations  2.47 us (2%)
    pallas_call x1, Pallas kernels, summed_gradient(): pl.pallas_call(functools.partial(kernel, nz, nx, slot, lines, tail_z, tai...  134 us
    unnamed x9, local copies, waits for them, and re-layouts  3.15 us

profile of v1, /device:TPU:65, one launch (start us, length us, event | category | flops | bytes accessed | tf_op | source)
XLA Modules:
  0.0 141.4 jit_solution(10727338123298552398)
XLA Ops:
  0.6 0.0 copy-start.1
  0.6 2.5 %copy.9.img_any = f32[512,448]{1,0:T(8,128)} copy(f32[512,448]{0,1:T(8,128)} %param.9) | data formatting | bytes 1835008 | tf_op args[3]
  3.1 0.0 copy-done.1
  3.1 0.6 pad_bitcast_fusion.par
  3.8 0.0 copy-start.3
  3.8 0.0 copy-start.2
  3.8 134.0 %shard_map.85 = f32[32,128]{1,0:T(8,128)} custom-call(f32[32,128]{1,0:T(8,128)} %pad_bitcast_fusion.par, s32[1,256]{1,0:T(1,128)} %idx.1, s32[1,512]{1,0:T(1,128)} %bitcast.13, f32[512,448]{1,0:T(8,128)} %copy.9.img_any), custom_call_target="tpu_custom_call" | custom-call | tf_op jit(solution)/shard_map/pallas_call | solution.py:387
  137.7 0.0 copy-done.3
  137.7 0.0 copy-start
  137.8 0.0 copy-done.2
  137.8 0.6 copy-done
  138.4 0.6 multiply_add_fusion
  139.1 0.5 slice.7
  (1 shorter events, 0.0 us)
Async XLA Ops:
  0.6 2.5 %copy-start.1 = (f32[3712]{0:T(1024)S(1)}, f32[3712]{0:T(1024)}, u32[]{:S(2)}) copy-start(f32[3712]{0:T(1024)} %param.6) | copy-start | bytes 44548
  3.8 134.0 %copy-start.3 = (f32[1,3712]{1,0:T(1,128)S(1)}, f32[1,3712]{1,0:T(1,128)}, u32[]{:S(2)}) copy-start(f32[1,3712]{1,0:T(1,128)} %param.8) | copy-start | bytes 44548
  3.8 134.0 %copy-start.2 = (f32[3712]{0:T(1024)S(1)}, f32[3712]{0:T(1024)}, u32[]{:S(2)}) copy-start(f32[3712]{0:T(1024)} %param.7) | copy-start | bytes 44548
  137.7 0.7 copy-start
